TPU v7x, 32 devices: a whole 2x2x4 slice. The times are simulated.
32 devices in a mesh: dom: 8 (over z, y), orb: 4 (over x, core).
Axes of the slice: x: 2, y: 2, z: 4, core: 2. Of those that a mesh axis runs over, the one named last changes fastest.
Arguments:
- orbitals: bfloat16 [16, 4, 1024, 512], P('dom', None, None, 'orb'), may hold values from -6 to 6
- slot_ids: int32 [16, 4], P('dom'), may hold values from 0 to 15, as said below
- slot_count: int32 [16], P('dom'), may hold values from 1 to 4, as said below
- band_tiles: bfloat16 [16, 3, 512, 512], P(None, None, 'dom', 'orb'), may hold values from -0.15625 to 0.15625
- pattern: int32 [16, 3], replicated, may hold values 0 or 1
- occupation: float32 [16, 512], P(None, 'orb'), may hold values from 0.0005 to 0.005
Outputs:
- rotated: bfloat16 [16, 4, 1024, 512], P('dom', None, None, 'orb')
- density: float32 [16, 1024], P('dom')
Inputs may be any that keep to these rules, and one draw needn't show every extreme that they name: `slot_ids`: each row names 4 consecutive orbital blocks counted modulo 16: slot l holds (s + l) mod 16, where the first block s of a grid block may be any of the 16 blocks. The slots in use on grid block g are its first slot_count[g]; some grid block uses all 4.
All inputs are finite; a program needn't handle non-finite values.
Results may differ from a plain program's by a relative error of at most 0.00094.
Values may be sent and summed in bfloat16 or wider, within the bound.
A program may use at most 128 MiB of HBM per device.

v0:
```python
import jax
import jax.numpy as jnp
from jax import lax
from jax.sharding import PartitionSpec as P


def select_tiles(band_full, pattern, slot_ids, slot_count):
    slots_per = slot_ids.shape[1]
    band_count = pattern.shape[1]
    half_band = (band_count - 1) // 2
    active = jnp.arange(slots_per, dtype=jnp.int32)[None, :] < slot_count[:, None]
    source = slot_ids[:, :, None]
    target = slot_ids[:, None, :]
    offset = target - source + half_band
    inside = (offset >= 0) & (offset < band_count)
    column = jnp.clip(offset, 0, band_count - 1)
    keeping = inside & (pattern[source, column] == 1) & active[:, :, None] & active[:, None, :]
    picked = band_full[source, column]
    return jnp.where(keeping[:, :, :, None, None], picked, jnp.zeros((), picked.dtype))


def rotate(values, tile_set):
    return jnp.einsum("glpi,glmij->gmpj", values, tile_set, preferred_element_type=jnp.float32)


def local(orbitals, slot_ids, slot_count, band_tiles, pattern, occupation):
    all_rows = lax.all_gather(band_tiles, "dom", axis=2, tiled=True)
    tile_set = select_tiles(all_rows, pattern, slot_ids, slot_count)
    rotated_f = rotate(lax.all_gather(orbitals, "orb", axis=3, tiled=True), tile_set)
    rotated = rotated_f.astype(jnp.bfloat16)
    onehot = (
        slot_ids[:, :, None] == jnp.arange(occupation.shape[0], dtype=jnp.int32)[None, None, :]
    ).astype(jnp.float32)
    weights = jnp.einsum("glb,bj->glj", onehot, occupation, precision=lax.Precision.HIGHEST)
    widened = rotated.astype(jnp.float32)
    square = widened * widened
    partial_density = jnp.einsum("gmpj,gmj->gp", square, weights, precision=lax.Precision.HIGHEST)
    density = lax.psum(partial_density, "orb")
    return (rotated, density)


def solution(mesh):
    placed = (
        P("dom", None, None, "orb"),
        P("dom", None),
        P("dom"),
        P(None, None, "dom", "orb"),
        P(),
        P(None, "orb"),
    )
    return jax.shard_map(
        local,
        mesh=mesh,
        in_specs=placed,
        out_specs=(P("dom", None, None, "orb"), P("dom", None)),
        check_vma=False,
    )
```

profile of v0, /device:TPU:0, one launch (start us, length us, event | category | flops | bytes accessed | tf_op | source)
XLA Modules:
  0.0 198.5 jit_solution(10908176028303874434)
XLA Ops:
  7.2 0.0 copy-start
  7.2 0.0 copy-start.2
  7.2 0.0 all-gather.3.cloned.1.call-start
  7.3 0.7 all-gather.3.cloned.1.call-update
  7.9 0.0 all-gather.5.cloned.1.call-start
  8.0 0.7 all-gather.5.cloned.1.call-update
  8.7 0.7 fusion.26
  9.4 0.8 fusion.17
  10.2 0.1 reshape.76
  10.3 0.8 gather_fusion
  11.1 0.1 reshape.89
  11.2 0.0 copy-done.3
  11.2 0.1 iota_compare_fusion.2
  11.2 0.1 fusion.23
  11.3 0.1 copy.11
  11.4 0.2 fusion.13
  11.7 100.0 %all-gather.3.cloned.1.call-done = bf16[16,3,512,128]{3,2,1,0:T(8,128)(2,1)} async-done(((bf16[16,3,64,128]{3,2,1,0:T(8,128)(2,1)}), bf16[16,3,512,128]{3,2,1,0:T(8,128)(2,1)}) %all-gather.3.cloned.1.call-update) | async-done | bytes 6291472 | tf_op jit(solution)/shard_map/all_gather | solution.py:27
  111.7 5.8 %gather_fusion.1 = bf16[32,512,128]{2,1,0:T(8,128)(2,1)} fusion(bf16[16,3,512,128]{3,2,1,0:T(8,128)(2,1)} %all-gather.3.cloned.1.call-done, s32[32]{0:T(128)S(1)} %reshape.76), kind=kCustom, calls=%fused_computation.1 | custom fusion | bytes 8388864 | tf_op jit(solution)/shard_map/gather | solution.py:18
  117.5 7.6 %copy.12 = bf16[2,4,4,512,128]{3,4,1,2,0:T(8,128)(2,1)} copy(bf16[2,4,4,512,128]{4,3,2,1,0:T(8,128)(2,1)} %bitcast.27) | data formatting | bytes 8388608 | tf_op jit(solution)/shard_map/gather | solution.py:18
  125.1 45.7 %all-gather.5.cloned.1.call-done = bf16[2,4,1024,512]{3,2,1,0:T(8,128)(2,1)} async-done(((bf16[2,4,1024,128]{3,2,1,0:T(8,128)(2,1)}), bf16[2,4,1024,512]{3,2,1,0:T(8,128)(2,1)}) %all-gather.5.cloned.1.call-update) | async-done | bytes 8388624 | tf_op jit(solution)/shard_map/all_gather | solution.py:29
  170.8 9.2 %fusion.7 = bf16[2,4,1024,128]{2,3,1,0:T(8,128)(2,1)S(1)} fusion(bf16[2,4,1024,512]{3,2,1,0:T(8,128)(2,1)} %all-gather.5.cloned.1.call-done, bf16[2,4,4,512,128]{3,4,1,2,0:T(8,128)(2,1)} %copy.12, pred[2,4,4]{1,2,0:T(4,128)(4,1)S(1)} %copy.11), kind=kOutput, calls=%fused_computation.10 | convolution fusion | flops 4298113024 | bytes 14680096 | tf_op jit(solution)/shard_map/glpi,glmij->gmpj/dot_general | solution.py:23
  180.0 2.6 %copy.13 = bf16[2,4,1024,128]{3,2,1,0:T(8,128)(2,1)} copy(bf16[2,4,1024,128]{2,3,1,0:T(8,128)(2,1)S(1)} %fusion.7) | data formatting | bytes 4194304
  182.6 2.5 %fusion.2 = f32[2,1,1024,1]{2,1,3,0:T(1,128)S(1)} fusion(f32[2,4,128,1]{2,3,1,0:T(1,128)S(1)} %bitcast.29, bf16[2,4,1024,128]{2,3,1,0:T(8,128)(2,1)S(1)} %fusion.7), kind=kOutput, calls=%fused_computation.5 | convolution fusion | flops 14680064 | bytes 2109440 | tf_op jit(solution)/shard_map/gmpj,gmj->gp/dot_general | solution.py:37
  185.1 6.6 %psum.7 = f32[2,1024]{1,0:T(2,128)} all-reduce(f32[2,1024]{1,0:T(2,128)S(1)} %bitcast.28), channel_id=1, replica_groups=mesh['dom'=8,'orb'=4] {'orb'}, use_global_device_ids=true, to_apply=%region_0.1 | all-reduce | flops 2048 | bytes 16384 | tf_op jit(solution)/shard_map/psum | solution.py:38
  (7 shorter events, 0.0 us)
Async XLA Ops:
  7.2 4.3 %copy-start = (f32[16,128]{1,0:T(8,128)S(1)}, f32[16,128]{1,0:T(8,128)}, u32[]{:S(2)}) copy-start(f32[16,128]{1,0:T(8,128)} %param.11) | copy-start | bytes 24580
  7.2 4.1 %copy-start.2 = (s32[2,4]{1,0:T(2,128)S(1)}, s32[2,4]{1,0:T(2,128)}, u32[]{:S(2)}) copy-start(s32[2,4]{1,0:T(2,128)} %param.7) | copy-start | bytes 100
  7.2 3.1 %copy-start.1 = (s32[16,3]{0,1:T(4,128)S(1)}, s32[16,3]{0,1:T(4,128)}, u32[]{:S(2)}) copy-start(s32[16,3]{0,1:T(4,128)} %param.10) | copy-start | bytes 580
  7.2 4.0 %copy-start.3 = (s32[2]{0:T(128)S(1)}, s32[2]{0:T(128)}, u32[]{:S(2)}) copy-start(s32[2]{0:T(128)} %param.8) | copy-start | bytes 28
  7.2 104.4 %all-gather.3.cloned.1.call-start = ((), (), s32[]{:S(2)}) async-start(), calls=%async_computation | async-start | bytes 7077888 | tf_op jit(solution)/shard_map/all_gather | solution.py:27
  7.9 162.9 %all-gather.5.cloned.1.call-start = ((), (), s32[]{:S(2)}) async-start(), calls=%async_computation.1 | async-start | bytes 10485760 | tf_op jit(solution)/shard_map/all_gather | solution.py:29
Sparse Core Ops, SparseCore 0:
  10.2 101.4 all-gather.2
  113.2 57.5 all-gather.4
where the time goes:
time: 199 us; the launch traced here: 198 us
  waiting for transfers between devices  147 us (74%)
  local copies, waits for them, and re-layouts  17.1 us (9%)
  between operations  14.1 us (7%)
  matrix products  11.9 us (6%)
  blocking collectives  6.59 us (3%)
    all_gather x1, waiting for transfers between devices, local(): all_rows = lax.all_gather(band_tiles, 'dom', axis=2, tiled=True)  100 us
    all_gather x1, waiting for transfers between devices, local(): lax.all_gather(orbitals, 'orb', axis=3, tiled=True)  45.7 us
    gather x2, local copies, waits for them, and re-layouts, select_tiles(): picked = band_full[source, column]  13.4 us
    dot_general x1, matrix products, rotate(): jnp.einsum('glpi,glmij->gmpj', values, tile_set, preferred_element_type=j...  9.19 us
    psum x1, blocking collectives, local(): density = lax.psum(partial_density, 'orb')  6.59 us
  transfers between devices with their start and end apart: 2, of which 2 were waited for; matrix products, arithmetic and copies ran while one was open for 8% of the time, Pallas kernels for 0%

commit v1 on v0

--- a/solution.py
+++ b/solution.py
@@ -26,7 +26,7 @@
 def local(orbitals, slot_ids, slot_count, band_tiles, pattern, occupation):
     all_rows = lax.all_gather(band_tiles, "dom", axis=2, tiled=True)
     tile_set = select_tiles(all_rows, pattern, slot_ids, slot_count)
-    rotated_f = rotate(lax.all_gather(orbitals, "orb", axis=3, tiled=True), tile_set)
+    rotated_f = rotate(jnp.concatenate(lax.all_gather(orbitals, "orb"), axis=3), tile_set)
     rotated = rotated_f.astype(jnp.bfloat16)
     onehot = (
         slot_ids[:, :, None] == jnp.arange(occupation.shape[0], dtype=jnp.int32)[None, None, :]

time: 199 us -> 223 us (1.12)
  local copies, waits for them, and re-layouts: 17.1 us -> 42.4 us
    reshape x0 -> x1, local copies, waits for them, and re-layouts: none -> 13.1 us  [local(): jnp.concatenate(lax.all_gather(orbitals, 'orb'), axis=3)]
    all_gather x0 -> x1, local copies, waits for them, and re-layouts: none -> 12.2 us  [local(): lax.all_gather(orbitals, 'orb')]
  transfers between devices with their start and end apart: 2 -> 2, of which waited for: 2 -> 2; matrix products, arithmetic and copies ran while one was open for 8% -> 7% of each run, Pallas kernels for 0% -> 0%
where the time goes in v1:
time: 223 us
  waiting for transfers between devices  146 us (65%)
  local copies, waits for them, and re-layouts  42.4 us (19%)
  between operations  14.1 us (6%)
  matrix products  11.9 us (5%)
  blocking collectives  6.59 us (3%)
    all_gather x1, waiting for transfers between devices, local(): all_rows = lax.all_gather(band_tiles, 'dom', axis=2, tiled=True)  100 us
    all_gather x1, waiting for transfers between devices, local(): lax.all_gather(orbitals, 'orb')  44.6 us
    gather x2, local copies, waits for them, and re-layouts, select_tiles(): picked = band_full[source, column]  13.4 us
    reshape x1, local copies, waits for them, and re-layouts, local(): jnp.concatenate(lax.all_gather(orbitals, 'orb'), axis=3)  13.1 us
    all_gather x1, local copies, waits for them, and re-layouts, local(): lax.all_gather(orbitals, 'orb')  12.2 us
    dot_general x1, matrix products, rotate(): jnp.einsum('glpi,glmij->gmpj', values, tile_set, preferred_element_type=j...  9.19 us
    psum x1, blocking collectives, local(): density = lax.psum(partial_density, 'orb')  6.59 us
  transfers between devices with their start and end apart: 2, of which 2 were waited for; matrix products, arithmetic and copies ran while one was open for 7% of the time, Pallas kernels for 0%

profile of v1, /device:TPU:0, one launch (start us, length us, event | category | flops | bytes accessed | tf_op | source)
XLA Modules:
  0.0 222.7 jit_solution(8748058482375309335)
XLA Ops:
  7.2 0.0 copy-start
  7.2 0.0 all-gather.4.cloned.1.call-start
  7.3 0.7 all-gather.4.cloned.1.call-update
  7.9 0.0 all-gather.6.cloned.1.call-start
  8.0 0.7 all-gather.6.cloned.1.call-update
  8.7 0.7 fusion.26
  9.4 0.8 fusion.17
  10.2 0.1 reshape.84
  10.3 0.8 gather_fusion
  11.1 0.1 reshape.98
  11.2 0.1 iota_compare_fusion.2
  11.2 0.1 fusion.23
  11.3 0.1 copy.16
  11.4 0.2 fusion.13
  11.7 100.0 %all-gather.4.cloned.1.call-done = bf16[16,3,512,128]{3,2,1,0:T(8,128)(2,1)} async-done(((bf16[16,3,64,128]{3,2,1,0:T(8,128)(2,1)}), bf16[16,3,512,128]{3,2,1,0:T(8,128)(2,1)}) %all-gather.4.cloned.1.call-update) | async-done | bytes 6291472 | tf_op jit(solution)/shard_map/all_gather | solution.py:27
  111.7 5.8 %gather_fusion.1 = bf16[32,512,128]{2,1,0:T(8,128)(2,1)} fusion(bf16[16,3,512,128]{3,2,1,0:T(8,128)(2,1)} %all-gather.4.cloned.1.call-done, s32[32]{0:T(128)S(1)} %reshape.84), kind=kCustom, calls=%fused_computation.1 | custom fusion | bytes 8388864 | tf_op jit(solution)/shard_map/gather | solution.py:18
  117.5 7.6 %copy.17 = bf16[2,4,4,512,128]{3,4,1,2,0:T(8,128)(2,1)} copy(bf16[2,4,4,512,128]{4,3,2,1,0:T(8,128)(2,1)} %bitcast.30) | data formatting | bytes 8388608 | tf_op jit(solution)/shard_map/gather | solution.py:18
  125.1 44.6 %all-gather.6.cloned.1.call-done = bf16[8,4,1024,128]{3,2,1,0:T(8,128)(2,1)} async-done(((bf16[2,4,1024,128]{3,2,1,0:T(8,128)(2,1)}), bf16[8,4,1024,128]{3,2,1,0:T(8,128)(2,1)}) %all-gather.6.cloned.1.call-update) | async-done | bytes 8388624 | tf_op jit(solution)/shard_map/all_gather | solution.py:29
  169.7 12.2 %copy.26 = bf16[4,2,4,1024,128]{4,0,3,2,1:T(4,128)(2,1)} copy(bf16[4,2,4,1024,128]{4,3,2,1,0:T(8,128)(2,1)} %bitcast.31) | data formatting | bytes 16777216 | tf_op jit(solution)/shard_map/all_gather | solution.py:29
  181.9 13.1 %reshape.99 = bf16[2,4,1024,512,1]{3,2,1,0,4:T(8,128)(2,1)} reshape(bf16[2,4,1024,4,128]{4,3,2,1,0:T(4,128)(2,1)} %bitcast.29) | data formatting | bytes 16777216 | tf_op jit(solution)/shard_map/reshape | solution.py:29
  195.0 9.2 %fusion.7 = bf16[2,4,1024,128]{2,3,1,0:T(8,128)(2,1)S(1)} fusion(bf16[2,4,1024,512,1]{3,2,1,0,4:T(8,128)(2,1)} %reshape.99, bf16[2,4,4,512,128]{3,4,1,2,0:T(8,128)(2,1)} %copy.17, pred[2,4,4]{1,2,0:T(4,128)(4,1)S(1)} %copy.16), kind=kOutput, calls=%fused_computation.11 | convolution fusion | flops 4298113024 | bytes 14680096 | tf_op jit(solution)/shard_map/glpi,glmij->gmpj/dot_general | solution.py:23
  204.2 2.6 %copy.19 = bf16[2,4,1024,128]{3,2,1,0:T(8,128)(2,1)} copy(bf16[2,4,1024,128]{2,3,1,0:T(8,128)(2,1)S(1)} %fusion.7) | data formatting | bytes 4194304
  206.7 2.5 %fusion.2 = f32[2,1,1024,1]{2,1,3,0:T(1,128)S(1)} fusion(f32[2,4,128,1]{2,3,1,0:T(1,128)S(1)} %bitcast.33, bf16[2,4,1024,128]{2,3,1,0:T(8,128)(2,1)S(1)} %fusion.7), kind=kOutput, calls=%fused_computation.6 | convolution fusion | flops 14680064 | bytes 2109440 | tf_op jit(solution)/shard_map/gmpj,gmj->gp/dot_general | solution.py:37
  209.2 6.6 %psum.7 = f32[2,1024]{1,0:T(2,128)} all-reduce(f32[2,1024]{1,0:T(2,128)S(1)} %bitcast.32), channel_id=1, replica_groups=mesh['dom'=8,'orb'=4] {'orb'}, use_global_device_ids=true, to_apply=%region_0.1 | all-reduce | flops 2048 | bytes 16384 | tf_op jit(solution)/shard_map/psum | solution.py:38
  (9 shorter events, 0.0 us)
Async XLA Ops:
  7.2 4.3 %copy-start = (f32[16,128]{1,0:T(8,128)S(1)}, f32[16,128]{1,0:T(8,128)}, u32[]{:S(2)}) copy-start(f32[16,128]{1,0:T(8,128)} %param.11) | copy-start | bytes 24580
  7.2 4.1 %copy-start.2 = (s32[2,4]{1,0:T(2,128)S(1)}, s32[2,4]{1,0:T(2,128)}, u32[]{:S(2)}) copy-start(s32[2,4]{1,0:T(2,128)} %param.7) | copy-start | bytes 100
  7.2 3.1 %copy-start.1 = (s32[16,3]{0,1:T(4,128)S(1)}, s32[16,3]{0,1:T(4,128)}, u32[]{:S(2)}) copy-start(s32[16,3]{0,1:T(4,128)} %param.10) | copy-start | bytes 580
  7.2 4.0 %copy-start.3 = (s32[2]{0:T(128)S(1)}, s32[2]{0:T(128)}, u32[]{:S(2)}) copy-start(s32[2]{0:T(128)} %param.8) | copy-start | bytes 28
  7.2 104.4 %all-gather.4.cloned.1.call-start = ((), (), s32[]{:S(2)}) async-start(), calls=%async_computation | async-start | bytes 7077888 | tf_op jit(solution)/shard_map/all_gather | solution.py:27
  7.9 161.7 %all-gather.6.cloned.1.call-start = ((), (), s32[]{:S(2)}) async-start(), calls=%async_computation.1 | async-start | bytes 10485760 | tf_op jit(solution)/shard_map/all_gather | solution.py:29
Sparse Core Ops, SparseCore 0:
  10.2 101.4 all-gather.3
  113.2 56.4 all-gather.5
